TPU v7x, 32 devices: a whole 2x2x4 slice. The times are simulated.
32 devices in a mesh: dp: 8 (over z, y), tensor: 4 (over x, core).
Axes of the slice: x: 2, y: 2, z: 4, core: 2. Of those that a mesh axis runs over, the one named last changes fastest.
Arguments:
- acts: bfloat16 [8, 2048, 1024], P('dp', 'tensor'), may hold values from -6 to 6
- grad_out: bfloat16 [8, 2048, 1024], P('dp', 'tensor'), may hold values from -6 to 6
- norm_gain: float32 [1024], replicated, may hold values from 0.5 to 1.5
- w_zx: bfloat16 [1024, 2, 2048], P('dp', None, 'tensor'), may hold values from -0.1875 to 0.1875
- w_bc: bfloat16 [1024, 256], P('dp'), may hold values from -0.1875 to 0.1875
- w_dt: bfloat16 [1024, 32], P('dp', 'tensor'), may hold values from -0.1875 to 0.1875
- w_out: bfloat16 [1024, 2048], P('dp', 'tensor'), may hold values from -0.125 to 0.125
- conv_x: float32 [4, 2048], replicated, may hold values from -3 to 3
- conv_x_bias: float32 [2048], replicated, may hold values from -0.5 to 0.5
- conv_bc: float32 [4, 256], replicated, may hold values from -3 to 3
- conv_bc_bias: float32 [256], replicated, may hold values from -0.5 to 0.5
- dt_bias: float32 [32], replicated, may hold values from -7 to -2
- a_log: float32 [32], replicated, may hold values from 0 to 2.77
- d_skip: float32 [32], replicated, may hold values from 0.5 to 1.5
- gate_gain: float32 [2048], replicated, may hold values from 0.5 to 1.5
Outputs:
- out_acts: bfloat16 [8, 2048, 1024], P('dp', 'tensor')
- grad_acts: float32 [8, 2048, 1024], P('dp', 'tensor')
- grad_norm_gain: float32 [1024], replicated
- grad_w_zx: float32 [1024, 2, 2048], P('dp', None, 'tensor')
- grad_w_bc: float32 [1024, 256], P('dp')
- grad_w_dt: float32 [1024, 32], P('dp', 'tensor')
- grad_w_out: float32 [1024, 2048], P('dp', 'tensor')
- grad_conv_x: float32 [4, 2048], replicated
- grad_conv_x_bias: float32 [2048], replicated
- grad_conv_bc: float32 [4, 256], replicated
- grad_conv_bc_bias: float32 [256], replicated
- grad_dt_bias: float32 [32], replicated
- grad_a_log: float32 [32], replicated
- grad_d_skip: float32 [32], replicated
- grad_gate_gain: float32 [2048], replicated
All inputs are finite; a program needn't handle non-finite values.
Results may differ from a plain program's by a relative error of at most 0.0096.
Values may be sent and summed in bfloat16 or wider, within the bound.
A program may use at most 192 MiB of HBM per device.

v0:
```python
import jax
import jax.numpy as jnp
from jax import lax
from jax.sharding import PartitionSpec as P

BLOCK_LEN = 256
EPSILON = 1e-05
FULL_PRECISION = lax.Precision.HIGHEST
CONTRACT_LAST = (((1,), (1,)), ((), ()))
CONTRACT_FIRST = (((0,), (0,)), ((), ()))


def causal_conv(values, conv_taps):
    tap_count = conv_taps.shape[0]
    length = values.shape[0]
    padded = jnp.pad(values, ((tap_count - 1, 0), (0, 0)))
    result = conv_taps[0] * padded[0:length]
    for offset in range(1, tap_count):
        result = result + conv_taps[offset] * padded[offset : offset + length]
    return result


def ssd_scan(x_heads, step_dt, decay_rate, b_mat, c_mat, block_size):
    length, head_count, head_width = x_heads.shape
    state_count = b_mat.shape[1]
    block_count = length // block_size
    x_blocks = x_heads.reshape(block_count, block_size, head_count, head_width)
    dt_blocks = step_dt.reshape(block_count, block_size, head_count)
    b_blocks = b_mat.reshape(block_count, block_size, state_count)
    c_blocks = c_mat.reshape(block_count, block_size, state_count)
    positions = jnp.arange(block_size)
    causal_mask = (positions[:, None] >= positions[None, :]).astype(jnp.float32)

    def step_block(state, inputs):
        x_block, dt_block, b_block, c_block = inputs
        cum_logs = jnp.cumsum(dt_block * decay_rate[None, :], axis=0)
        scores = jnp.dot(c_block, b_block.T, precision=FULL_PRECISION)
        log_gaps = (cum_logs[:, None, :] - cum_logs[None, :, :]) * causal_mask[:, :, None]
        weights = (
            scores[:, :, None] * jnp.exp(log_gaps) * causal_mask[:, :, None] * dt_block[None, :, :]
        )
        within = jnp.einsum("ijh,jhp->ihp", weights, x_block, precision=FULL_PRECISION)
        carried = (
            jnp.einsum("in,hpn->ihp", c_block, state, precision=FULL_PRECISION)
            * jnp.exp(cum_logs)[:, :, None]
        )
        block_total = cum_logs[-1]
        state_weight = jnp.exp(block_total[None, :] - cum_logs) * dt_block
        update = jnp.einsum(
            "jhp,jn->hpn", x_block * state_weight[:, :, None], b_block, precision=FULL_PRECISION
        )
        new_state = state * jnp.exp(block_total)[:, None, None] + update
        return (new_state, within + carried)

    zero_state = jnp.zeros((head_count, head_width, state_count), jnp.float32)
    final_state, outputs = lax.scan(
        jax.checkpoint(step_block), zero_state, (x_blocks, dt_blocks, b_blocks, c_blocks)
    )
    return outputs.reshape(length, head_count, head_width)


def pre_norm(acts_row, norm_gain):
    return (
        acts_row
        * lax.rsqrt(jnp.mean(acts_row * acts_row, axis=-1, keepdims=True) + EPSILON)
        * norm_gain
    )


def conv_part(x_vals, bc_vals, x_taps, x_shift, bc_taps, bc_shift):
    x_conv = jax.nn.silu(causal_conv(x_vals, x_taps) + x_shift)
    bc_conv = jax.nn.silu(causal_conv(bc_vals, bc_taps) + bc_shift)
    return (x_conv, bc_conv)


def mix_part(x_vals, b_vals, c_vals, dt_vals, dt_shift, log_rate, skip_gain, gate_vals):
    length = x_vals.shape[0]
    head_count = dt_vals.shape[1]
    x_heads = x_vals.reshape(length, head_count, -1)
    step_dt = jax.nn.softplus(dt_vals + dt_shift)
    mixed = (
        ssd_scan(x_heads, step_dt, -jnp.exp(log_rate), b_vals, c_vals, BLOCK_LEN)
        + skip_gain[None, :, None] * x_heads
    )
    return mixed.reshape(length, -1) * jax.nn.silu(gate_vals)


def widen(piece, start, full_size):
    holder = jnp.zeros(piece.shape[:-1] + (full_size,), jnp.float32)
    return lax.dynamic_update_slice_in_dim(holder, piece, start, piece.ndim - 1)


def body(
    acts,
    grad_out,
    norm_gain,
    w_zx,
    w_bc,
    w_dt,
    w_out,
    conv_x,
    conv_x_bias,
    conv_bc,
    conv_bc_bias,
    dt_bias,
    a_log,
    d_skip,
    gate_gain,
):
    parts = lax.axis_size("tensor")
    rank = lax.axis_index("tensor")
    local_rows = acts.shape[1]
    channels = w_zx.shape[2]
    head_count = w_dt.shape[1]
    state_count = w_bc.shape[1] // 2
    total_channels = channels * parts
    total_heads = head_count * parts
    chan_start = rank * channels
    head_start = rank * head_count
    zx_full, bc_full, dt_full, out_full = (
        lax.all_gather(w_zx, "dp", axis=0, tiled=True),
        lax.all_gather(w_bc, "dp", axis=0, tiled=True),
        lax.all_gather(w_dt, "dp", axis=0, tiled=True),
        lax.all_gather(w_out, "dp", axis=0, tiled=True),
    )
    acts_row = acts[0].astype(jnp.float32)
    normed_in, pre_back = jax.vjp(pre_norm, acts_row, norm_gain)
    hidden = lax.all_gather(normed_in.astype(jnp.bfloat16), "tensor", axis=0, tiled=True)
    zx_proj = jnp.einsum("ld,dkc->lkc", hidden, zx_full, preferred_element_type=jnp.float32)
    bc_proj = jnp.dot(hidden, bc_full, preferred_element_type=jnp.float32)
    dt_proj = jnp.dot(hidden, dt_full, preferred_element_type=jnp.float32)
    conv_x_local = lax.dynamic_slice_in_dim(conv_x, chan_start, channels, 1)
    conv_xb_local = lax.dynamic_slice_in_dim(conv_x_bias, chan_start, channels, 0)
    dt_bias_local = lax.dynamic_slice_in_dim(dt_bias, head_start, head_count, 0)
    a_log_local = lax.dynamic_slice_in_dim(a_log, head_start, head_count, 0)
    d_skip_local = lax.dynamic_slice_in_dim(d_skip, head_start, head_count, 0)
    gain_local = lax.dynamic_slice_in_dim(gate_gain, chan_start, channels, 0)
    conv_outs, conv_back = jax.vjp(
        conv_part, zx_proj[:, 1], bc_proj, conv_x_local, conv_xb_local, conv_bc, conv_bc_bias
    )
    x_conv, bc_conv = conv_outs
    x_low = x_conv.astype(jnp.bfloat16)
    b_low = bc_conv[:, :state_count].astype(jnp.bfloat16)
    c_low = bc_conv[:, state_count:].astype(jnp.bfloat16)
    gated, mix_back = jax.vjp(
        mix_part,
        x_low.astype(jnp.float32),
        b_low.astype(jnp.float32),
        c_low.astype(jnp.float32),
        dt_proj,
        dt_bias_local,
        a_log_local,
        d_skip_local,
        zx_proj[:, 0],
    )
    square_total = lax.psum(jnp.sum(gated * gated, axis=1), "tensor")
    inv_rms = lax.rsqrt(square_total / total_channels + EPSILON)[:, None]
    mixed_out = (gated * inv_rms * gain_local).astype(jnp.bfloat16)
    projected = lax.psum_scatter(
        lax.dot_general(mixed_out, out_full, CONTRACT_LAST, preferred_element_type=jnp.float32),
        "tensor",
        scatter_dimension=0,
        tiled=True,
    )
    out_acts = (acts_row + projected).astype(jnp.bfloat16)[None]
    grad_row = grad_out[0]
    grad_rows_all = lax.all_gather(grad_row, "tensor", axis=0, tiled=True)
    grad_mixed = jnp.dot(grad_rows_all, out_full, preferred_element_type=jnp.float32).astype(
        jnp.bfloat16
    )
    grad_out_w = lax.dot_general(
        grad_rows_all, mixed_out, CONTRACT_FIRST, preferred_element_type=jnp.float32
    )
    grad_normed = grad_mixed.astype(jnp.float32)
    grad_gain_local = jnp.sum(grad_normed * gated * inv_rms, axis=0)
    scaled = grad_normed * gain_local
    row_dot = lax.psum(jnp.sum(scaled * gated, axis=1), "tensor")
    grad_gated = (
        inv_rms * scaled
        - gated * (inv_rms * inv_rms * inv_rms) * (row_dot / total_channels)[:, None]
    )
    (
        grad_x_low,
        grad_b,
        grad_c,
        grad_dt_in,
        grad_dt_shift,
        grad_log_rate,
        grad_skip,
        grad_gate_in,
    ) = mix_back(grad_gated)
    grad_x_in, grad_bc_part, grad_x_taps, grad_x_shift, grad_bc_taps, grad_bc_shift = conv_back(
        (grad_x_low, jnp.concatenate([grad_b, grad_c], axis=1))
    )
    grad_bc_in = lax.psum(grad_bc_part, "tensor").astype(jnp.bfloat16)
    grad_zx = jnp.stack([grad_gate_in.astype(jnp.bfloat16), grad_x_in.astype(jnp.bfloat16)], axis=1)
    grad_dt_low = grad_dt_in.astype(jnp.bfloat16)
    grad_zx_w = jnp.einsum("ld,lkc->dkc", hidden, grad_zx, preferred_element_type=jnp.float32)
    grad_bc_w = lax.dot_general(
        hidden, grad_bc_in, CONTRACT_FIRST, preferred_element_type=jnp.float32
    )
    grad_dt_w = lax.dot_general(
        hidden, grad_dt_low, CONTRACT_FIRST, preferred_element_type=jnp.float32
    )
    from_zx = jnp.einsum("lkc,dkc->ld", grad_zx, zx_full, preferred_element_type=jnp.float32)
    grad_hidden = lax.psum_scatter(
        from_zx
        + lax.dot_general(grad_dt_low, dt_full, CONTRACT_LAST, preferred_element_type=jnp.float32),
        "tensor",
        scatter_dimension=0,
        tiled=True,
    )
    bc_piece = lax.dynamic_slice_in_dim(grad_bc_in, rank * local_rows, local_rows, 0)
    grad_hidden = grad_hidden + lax.dot_general(
        bc_piece, bc_full, CONTRACT_LAST, preferred_element_type=jnp.float32
    )
    grad_acts_norm, grad_norm_gain = pre_back(grad_hidden)
    grad_acts = (grad_row.astype(jnp.float32) + grad_acts_norm)[None]
    grad_w_zx, grad_w_bc, grad_w_dt, grad_w_out = (
        lax.psum_scatter(grad_zx_w, "dp", scatter_dimension=0, tiled=True),
        lax.psum_scatter(grad_bc_w, "dp", scatter_dimension=0, tiled=True),
        lax.psum_scatter(grad_dt_w, "dp", scatter_dimension=0, tiled=True),
        lax.psum_scatter(grad_out_w, "dp", scatter_dimension=0, tiled=True),
    )
    small_sums = lax.psum(
        (
            grad_norm_gain,
            widen(grad_x_taps, chan_start, total_channels),
            widen(grad_x_shift, chan_start, total_channels),
            grad_bc_taps,
            grad_bc_shift,
            widen(grad_dt_shift, head_start, total_heads),
            widen(grad_log_rate, head_start, total_heads),
            widen(grad_skip, head_start, total_heads),
            widen(grad_gain_local, chan_start, total_channels),
        ),
        ("dp", "tensor"),
    )
    grad_ng, grad_cx, grad_cxb, grad_cbc, grad_cbcb, grad_dtb, grad_alog, grad_dsk, grad_gg = (
        small_sums
    )
    return (
        out_acts,
        grad_acts,
        grad_ng,
        grad_w_zx,
        grad_w_bc,
        grad_w_dt,
        grad_w_out,
        grad_cx,
        grad_cxb,
        grad_cbc,
        grad_cbcb,
        grad_dtb,
        grad_alog,
        grad_dsk,
        grad_gg,
    )


def solution(mesh):
    in_specs = (
        P("dp", "tensor", None),
        P("dp", "tensor", None),
        P(),
        P("dp", None, "tensor"),
        P("dp", None),
        P("dp", "tensor"),
        P("dp", "tensor"),
        P(),
        P(),
        P(),
        P(),
        P(),
        P(),
        P(),
        P(),
    )
    out_specs = (
        P("dp", "tensor", None),
        P("dp", "tensor", None),
        P(),
        P("dp", None, "tensor"),
        P("dp", None),
        P("dp", "tensor"),
        P("dp", "tensor"),
        P(),
        P(),
        P(),
        P(),
        P(),
        P(),
        P(),
        P(),
    )
    return jax.shard_map(body, mesh=mesh, in_specs=in_specs, out_specs=out_specs, check_vma=False)
```

profile of v0, /device:TPU:0, one launch (start us, length us, event | category | flops | bytes accessed | tf_op | source)
XLA Modules:
  0.0 918.6 jit_solution(7278153467009917441)
XLA Ops:
  16.2 27.9 %all_gather.19 = bf16[1024,8]{0,1:T(8,128)(2,1)S(1)} all-gather(bf16[128,8]{0,1:T(8,128)(2,1)S(1)} %copy-done.49), channel_id=1, replica_groups=mesh['dp'=8,'tensor'=4] {'dp'}, dimensions={0}, use_global_device_ids=true | all-gather | bytes 18432 | tf_op jit(solution)/shard_map/all_gather | solution.py:123
  44.2 32.4 %all_gather.21 = bf16[1024,256]{1,0:T(8,128)(2,1)S(1)} all-gather(bf16[128,256]{1,0:T(8,128)(2,1)S(1)} %copy-done.20), channel_id=1, replica_groups=mesh['dp'=8,'tensor'=4] {'dp'}, dimensions={0}, use_global_device_ids=true | all-gather | bytes 589824 | tf_op jit(solution)/shard_map/all_gather | solution.py:122
  77.6 3.8 fusion.161
  86.3 15.2 %all-gather.8.cloned.1.call-done = bf16[1024,2,512]{2,0,1:T(8,128)(2,1)} async-done(((bf16[128,2,512]{2,0,1:T(8,128)(2,1)}), bf16[1024,2,512]{2,0,1:T(8,128)(2,1)}) %all-gather.8.cloned.1.call-update) | async-done | bytes 2097168 | tf_op jit(solution)/shard_map/all_gather | solution.py:121
  101.5 7.1 fusion.109
  112.3 4.7 fusion.123
  117.0 7.1 reshape.372
  124.1 6.9 copy.89
  130.9 4.0 compare_select_fusion.2
  137.4 87.5 %while.43 = (s32[]{:T(128)}, f32[8,64,128]{2,1,0:T(8,128)S(1)}, f32[8,256,8,64]{1,3,2,0:T(8,128)}, f32[8,8,64,128]{3,2,1,0:T(8,128)}, f32[8,256,8]{1,2,0:T(8,128...) while((s32[]{:T(128)}, f32[8,64,128]{2,1,0:T(8,128)S(1)}, ...), condition=%wide.region_4.5_spmd.clone.clone, body=%wide.region_1.4_spmd.clone.clone.sunk | while | flops 909711360 | bytes 5641051 | solution.py:56
  140.0 3.6 fusion.270
  150.9 3.6 fusion.270
  161.9 3.6 fusion.270
  172.9 3.6 fusion.270
  183.8 3.6 fusion.270
  194.7 3.6 fusion.270
  205.7 3.6 fusion.270
  216.6 3.6 fusion.270
  225.0 6.9 copy.101
  231.9 7.5 reshape.369
  239.4 7.6 multiply_reduce_fusion.8
  246.9 5.7 psum.84
  252.7 7.2 fusion.130
  260.0 7.4 fusion.96
  267.5 6.8 psum.85
  274.3 11.7 %multiply_reduce_fusion.3 = (f32[512]{0:T(512)}, f32[2048,512]{1,0:T(8,128)}, bf16[2048,1,512]{2,0,1:T(8,128)(2,1)}) fusion(f32[2048,512]{1,0:T(8,128)} %get-tuple-element.766, f32[2048,2,512]{2,0,1:T(8,128)} %copy-done.1, f32[2048]{0:T(1024)S(1)} %broadcast_multiply_fusion.8, f32[2048,512]{1,0:T(8,128)} %get-tuple-element.762, ...), kind=kLoop, calls=%fused_computation.161 | loop fusion | flops 30408192 | bytes 25196544 | tf_op jit(solution)/shard_map/transpose(jvp())/reduce_sum | solution.py:83
  286.0 7.1 reshape.370
  293.1 6.8 copy.94
  305.2 198.0 %while.42 = (s32[]{:T(128)}, f32[8]{0:T(128)}, f32[8,64,128]{2,1,0:T(8,128)S(1)}, f32[8,256,8,64]{1,3,2,0:T(8,128)}, f32[8,256,8]{1,2,0:T(8,128)}, /*index=5*/f3...) while((s32[]{:T(128)}, f32[8]{0:T(128)}, ...), condition=%wide.region_24.25_spmd.clone, body=%wide.region_10.0_spmd.clone.sunk | while | flops 2126610432 | bytes 15952340 | solution.py:56
  337.4 3.4 fusion.252
  411.8 3.4 fusion.252
  503.2 6.9 copy.104
  510.1 7.5 reshape.371
  517.7 11.5 %multiply_reduce_fusion.6 = (f32[512]{0:T(512)S(1)}, f32[512]{0:T(512)S(1)}, f32[512]{0:T(512)S(1)}, f32[512]{0:T(512)S(1)}, f32[512]{0:T(512)S(1)}, /*index=5*/f32[2048,512]{1,0:T(8,128)S(1)}) fusion(f32[2048,512]{1,0:T(8,128)} %copy-done, f32[2048,2,512]{2,0,1:T(8,128)} %copy-done.1, f32[2048,512]{1,0:T(8,128)} %get-tuple-element.766, ...), kind=kLoop, calls=%fused_computation.164 | loop fusion | flops 20968960 | bytes 25178112 | tf_op jit(solution)/shard_map/transpose(jvp())/reduce_sum | solution.py:19
  529.2 5.8 broadcast_multiply_fusion
  535.0 7.1 fusion.127
  542.2 8.2 fusion.107
  554.3 6.8 bitcast_add_fusion
  562.4 7.8 fusion.148
  579.6 40.8 %all-reduce.21 = bf16[2048,256]{1,0:T(8,128)(2,1)S(1)} all-reduce(f32[2048,256]{1,0:T(8,128)S(1)} %pad_add_fusion.3), channel_id=1, replica_groups=mesh['dp'=8,'tensor'=4] {'tensor'}, use_global_device_ids=true, to_apply=%region_26.27 | all-reduce | flops 524288 | bytes 3145728 | tf_op jit(solution)/shard_map/psum | solution.py:195
  620.5 4.9 fusion.162
  628.7 8.8 reduce-scatter.11.cloned.1.call-done
  639.7 71.4 %reduce-scatter.9.cloned.1.call-done = f32[512,1024]{1,0:T(8,128)} async-done(((f32[2048,1024]{1,0:T(8,128)}), f32[512,1024]{1,0:T(8,128)}) %reduce-scatter.9.cloned.1.call-update) | async-done | bytes 2097168 | tf_op jit(solution)/shard_map/reduce_scatter | solution.py:206
  713.8 41.1 %all-reduce.19 = (f32[1024]{0:T(1024)}, f32[4,2048]{1,0:T(4,128)}, f32[2048]{0:T(1024)}, f32[4,256]{1,0:T(4,128)}, f32[256]{0:T(256)}, /*index=5*/f32[32]{0:T(128)}, f32[32]{0:T(128)}, f32[32]{0:T(128)}, f32[2048]{0:T(1024)}) all-reduce(f32[1024]{0:T(1024)S(1)} %get-tuple-element.689, ...), channel_id=1, replica_groups=mesh['dp'=8,'tensor'=4] {'dp','tensor'}, use_global_device_ids=true, to_apply=%region_29.30 | all-reduce | flops 14688 | bytes 117504 | tf_op jit(solution)/shard_map/psum | solution.py:225
  754.9 30.9 %reduce-scatter.7.cloned.1.call-done = f32[512,1024]{1,0:T(8,128)} async-done(((f32[2048,1024]{1,0:T(8,128)}), f32[512,1024]{1,0:T(8,128)}) %reduce-scatter.7.cloned.1.call-update) | async-done | bytes 2097168 | tf_op jit(solution)/shard_map/reduce_scatter | solution.py:159
  785.8 4.3 fusion.122
  790.0 54.2 %reduce-scatter.15.cloned.1.call-done = f32[128,8]{0,1:T(8,128)} async-done(((f32[1024,8]{0,1:T(8,128)}), f32[128,8]{0,1:T(8,128)}) %reduce-scatter.15.cloned.1.call-update) | async-done | bytes 4112 | tf_op jit(solution)/shard_map/reduce_scatter | solution.py:222
  844.3 67.1 %reduce-scatter.13.cloned.1.call-done = f32[128,256]{1,0:T(8,128)} async-done(((f32[1024,256]{1,0:T(8,128)}), f32[128,256]{1,0:T(8,128)}) %reduce-scatter.13.cloned.1.call-update) | async-done | bytes 131088 | tf_op jit(solution)/shard_map/reduce_scatter | solution.py:221
  (599 shorter events, 297.5 us)
Async XLA Ops:
  7.2 6.4 copy-start.52
  7.2 7.1 copy-start.55
  7.2 7.2 copy-start.56
  7.2 8.9 copy-start.48
  7.2 8.9 copy-start.49
  7.2 36.9 %copy-start.20 = (bf16[128,256]{1,0:T(8,128)(2,1)S(1)}, bf16[128,256]{1,0:T(8,128)(2,1)}, u32[]{:S(2)}) copy-start(bf16[128,256]{1,0:T(8,128)(2,1)} %param.23) | copy-start | bytes 196612
  7.3 70.3 %all-gather.6.cloned.1.call-start = ((), (), s32[]{:S(2)}) async-start(), calls=%async_computation.6 | async-start | bytes 5242880 | tf_op jit(solution)/shard_map/all_gather | solution.py:128
  8.9 7.3 copy-start.36
  8.9 7.3 copy-start.24
  11.4 90.1 %all-gather.8.cloned.1.call-start = ((), (), s32[]{:S(2)}) async-start(), calls=%async_computation.7 | async-start | bytes 2359296 | tf_op jit(solution)/shard_map/all_gather | solution.py:121
  12.2 240.5 %all-gather.12.cloned.1.call-start = ((), (), s32[]{:S(2)}) async-start(), calls=%async_computation.15 | async-start | bytes 5242880 | tf_op jit(solution)/shard_map/all_gather | solution.py:167
  13.0 247.0 %all-gather.10.cloned.1.call-start = ((), (), s32[]{:S(2)}) async-start(), calls=%async_computation.8 | async-start | bytes 1179648 | tf_op jit(solution)/shard_map/all_gather | solution.py:124
  13.6 613.3 %reduce-scatter.17.cloned.1.call-start = ((), (), s32[]{:S(2)}) async-start(), calls=%async_computation.14 | async-start | bytes 2359296 | tf_op jit(solution)/shard_map/reduce_scatter | solution.py:223
  15.2 259.0 %copy-start.26 = (f32[512]{0:T(512)}, f32[512]{0:T(512)S(1)}, u32[]{:S(2)}) copy-start(f32[512]{0:T(512)S(1)} %dynamic_slice.100) | copy-start | bytes 6148
  16.1 258.1 %copy-start.22 = (f32[512]{0:T(512)}, f32[512]{0:T(512)S(1)}, u32[]{:S(2)}) copy-start(f32[512]{0:T(512)S(1)} %mul.863) | copy-start | bytes 6148
  16.2 65.2 %copy-start.39 = (f32[1,256]{1,0:T(1,128)}, f32[1,256]{1,0:T(1,128)S(1)}, u32[]{:S(2)}) copy-start(f32[1,256]{1,0:T(1,128)S(1)} %get-tuple-element.793) | copy-start | bytes 3076
  16.2 65.2 %copy-start.41 = (f32[1,256]{1,0:T(1,128)}, f32[1,256]{1,0:T(1,128)S(1)}, u32[]{:S(2)}) copy-start(f32[1,256]{1,0:T(1,128)S(1)} %get-tuple-element.794) | copy-start | bytes 3076
  16.2 65.2 %copy-start.43 = (f32[1,256]{1,0:T(1,128)}, f32[1,256]{1,0:T(1,128)S(1)}, u32[]{:S(2)}) copy-start(f32[1,256]{1,0:T(1,128)S(1)} %get-tuple-element.795) | copy-start | bytes 3076
  16.2 65.2 %copy-start.45 = (f32[1,256]{1,0:T(1,128)}, f32[1,256]{1,0:T(1,128)S(1)}, u32[]{:S(2)}) copy-start(f32[1,256]{1,0:T(1,128)S(1)} %get-tuple-element.796) | copy-start | bytes 3076
  44.1 86.8 %copy-start.18 = (bf16[1024,8]{0,1:T(8,128)(2,1)}, bf16[1024,8]{0,1:T(8,128)(2,1)S(1)}, u32[]{:S(2)}) copy-start(bf16[1024,8]{0,1:T(8,128)(2,1)S(1)} %all_gather.19) | copy-start | bytes 49156
  44.2 37.3 %copy-start.51 = (f32[256]{0:T(256)S(1)}, f32[256]{0:T(256)}, u32[]{:S(2)}) copy-start(f32[256]{0:T(256)} %param.29) | copy-start | bytes 3076
  76.6 4.8 copy-start.10
  77.5 34.7 %copy-start.28 = (f32[1,512]{1,0:T(1,128)}, f32[1,512]{1,0:T(1,128)S(1)}, u32[]{:S(2)}) copy-start(f32[1,512]{1,0:T(1,128)S(1)} %get-tuple-element.787) | copy-start | bytes 6148
  77.5 34.7 %copy-start.30 = (f32[1,512]{1,0:T(1,128)}, f32[1,512]{1,0:T(1,128)S(1)}, u32[]{:S(2)}) copy-start(f32[1,512]{1,0:T(1,128)S(1)} %get-tuple-element.788) | copy-start | bytes 6148
  77.6 34.7 %copy-start.32 = (f32[1,512]{1,0:T(1,128)}, f32[1,512]{1,0:T(1,128)S(1)}, u32[]{:S(2)}) copy-start(f32[1,512]{1,0:T(1,128)S(1)} %get-tuple-element.789) | copy-start | bytes 6148
  77.6 34.7 %copy-start.34 = (f32[1,512]{1,0:T(1,128)}, f32[1,512]{1,0:T(1,128)S(1)}, u32[]{:S(2)}) copy-start(f32[1,512]{1,0:T(1,128)S(1)} %get-tuple-element.790) | copy-start | bytes 6148
  112.3 4.7 copy-start
  252.7 21.6 %copy-start.16 = (f32[2048]{0:T(1024)}, f32[2048]{0:T(1024)S(1)}, u32[]{:S(2)}) copy-start(f32[2048]{0:T(1024)S(1)} %get-tuple-element.792) | copy-start | bytes 24580
  260.0 377.4 %reduce-scatter.11.cloned.1.call-start = ((), (), s32[]{:S(2)}) async-start(), calls=%async_computation.11 | async-start | bytes 4718592 | tf_op jit(solution)/shard_map/reduce_scatter | solution.py:220
  510.1 7.5 copy-start.23
  517.6 11.6 %copy-start.29 = (f32[1,512]{1,0:T(1,128)S(1)}, f32[1,512]{1,0:T(1,128)}, u32[]{:S(2)}) copy-start(f32[1,512]{1,0:T(1,128)} %copy-done.28) | copy-start | bytes 6148
  517.6 11.6 %copy-start.31 = (f32[1,512]{1,0:T(1,128)S(1)}, f32[1,512]{1,0:T(1,128)}, u32[]{:S(2)}) copy-start(f32[1,512]{1,0:T(1,128)} %copy-done.30) | copy-start | bytes 6148
  517.6 11.6 %copy-start.33 = (f32[1,512]{1,0:T(1,128)S(1)}, f32[1,512]{1,0:T(1,128)}, u32[]{:S(2)}) copy-start(f32[1,512]{1,0:T(1,128)} %copy-done.32) | copy-start | bytes 6148
  517.6 11.6 %copy-start.35 = (f32[1,512]{1,0:T(1,128)S(1)}, f32[1,512]{1,0:T(1,128)}, u32[]{:S(2)}) copy-start(f32[1,512]{1,0:T(1,128)} %copy-done.34) | copy-start | bytes 6148
  535.0 7.2 copy-start.2
  550.4 160.6 %reduce-scatter.9.cloned.1.call-start = ((), (), s32[]{:S(2)}) async-start(), calls=%async_computation.10 | async-start | bytes 10485760 | tf_op jit(solution)/shard_map/reduce_scatter | solution.py:206
  561.2 224.6 %reduce-scatter.7.cloned.1.call-start = ((), (), s32[]{:S(2)}) async-start(), calls=%async_computation.9 | async-start | bytes 10485760 | tf_op jit(solution)/shard_map/reduce_scatter | solution.py:159
  570.2 274.0 %reduce-scatter.15.cloned.1.call-start = ((), (), s32[]{:S(2)}) async-start(), calls=%async_computation.13 | async-start | bytes 36864 | tf_op jit(solution)/shard_map/reduce_scatter | solution.py:222
  620.4 5.1 copy-start.11
  620.4 5.1 copy-start.47
  620.4 5.1 copy-start.50
  620.4 6.2 copy-start.38
  620.4 6.2 copy-start.53
  620.4 90.6 %copy-start.4 = (bf16[1,512,1024]{2,1,0:T(8,128)(2,1)S(1)}, bf16[1,512,1024]{2,1,0:T(8,128)(2,1)}, u32[]{:S(2)}) copy-start(bf16[1,512,1024]{2,1,0:T(8,128)(2,1)} %param.19) | copy-start | bytes 3145732
  620.5 90.6 %copy-start.21 = (f32[1024]{0:T(1024)S(1)}, f32[1024]{0:T(1024)}, u32[]{:S(2)}) copy-start(f32[1024]{0:T(1024)} %param.21) | copy-start | bytes 12292
  620.5 90.6 %copy-start.25 = (f32[512]{0:T(512)S(1)}, f32[512]{0:T(512)}, u32[]{:S(2)}) copy-start(f32[512]{0:T(512)} %copy-done.24) | copy-start | bytes 6148
  620.5 290.9 %reduce-scatter.13.cloned.1.call-start = ((), (), s32[]{:S(2)}) async-start(), calls=%async_computation.12 | async-start | bytes 1179648 | tf_op jit(solution)/shard_map/reduce_scatter | solution.py:221
  625.4 129.5 %copy-start.37 = (f32[512]{0:T(512)S(1)}, f32[512]{0:T(512)}, u32[]{:S(2)}) copy-start(f32[512]{0:T(512)} %copy-done.36) | copy-start | bytes 6148
  (19 other events, 43.6 us)
Sparse Core Ops, SparseCore 0:
  11.6 37.1 all-gather.5
  51.5 49.9 all-gather.7
  103.1 32.9 all-gather.11
  138.1 40.3 all-gather.9
  260.1 68.2 reduce-scatter.16
  550.6 86.8 reduce-scatter.10
  640.0 71.0 reduce-scatter.8
  713.6 72.0 reduce-scatter.6
  789.5 54.7 reduce-scatter.14
  848.1 63.1 reduce-scatter.12
where the time goes:
time: 926 us; the launch traced here: 919 us
  waiting for transfers between devices  249 us (27%)
  matrix products  235 us (25%)
  blocking collectives  155 us (17%)
  other arithmetic  140 us (15%)
  local copies, waits for them, and re-layouts  123 us (13%)
  between operations  15.3 us (2%)
    dot_general x24, matrix products, step_block(): jnp.einsum('ijh,jhp->ihp', weights, x_block, precision=FULL_PRECISION)  78.3 us
    reduce_scatter x1, waiting for transfers between devices, body(): lax.psum_scatter(from_zx + lax.dot_general(grad_dt_low, dt_full, CONTRACT...  71.4 us
    reduce_scatter x1, waiting for transfers between devices, body(): lax.psum_scatter(grad_bc_w, 'dp', scatter_dimension=0, tiled=True)  67.1 us
    reduce_scatter x1, waiting for transfers between devices, body(): lax.psum_scatter(grad_dt_w, 'dp', scatter_dimension=0, tiled=True)  54.2 us
    psum x1, blocking collectives, body(): lax.psum((grad_norm_gain, widen(grad_x_taps, chan_start, total_channels),...  41.1 us
    psum x1, blocking collectives, body(): grad_bc_in = lax.psum(grad_bc_part, 'tensor').astype(jnp.bfloat16)  40.8 us
    another operation x73, other arithmetic  39.1 us
    dot_general x32, matrix products, step_block(): jnp.einsum('in,hpn->ihp', c_block, state, precision=FULL_PRECISION)  35.8 us
  transfers between devices with their start and end apart: 10, of which 6 were waited for; matrix products, arithmetic and copies ran while one was open for 53% of the time, Pallas kernels for 0%

commit v1 on v0

--- a/solution.py
+++ b/solution.py
@@ -192,7 +192,10 @@
     grad_x_in, grad_bc_part, grad_x_taps, grad_x_shift, grad_bc_taps, grad_bc_shift = conv_back(
         (grad_x_low, jnp.concatenate([grad_b, grad_c], axis=1))
     )
-    grad_bc_in = lax.psum(grad_bc_part, "tensor").astype(jnp.bfloat16)
+    positions_drive = lambda local_values, row_axis: lax.all_gather(local_values, row_axis).sum(
+        axis=0
+    )
+    grad_bc_in = positions_drive(grad_bc_part, "tensor").astype(jnp.bfloat16)
     grad_zx = jnp.stack([grad_gate_in.astype(jnp.bfloat16), grad_x_in.astype(jnp.bfloat16)], axis=1)
     grad_dt_low = grad_dt_in.astype(jnp.bfloat16)
     grad_zx_w = jnp.einsum("ld,lkc->dkc", hidden, grad_zx, preferred_element_type=jnp.float32)

time: 926 us -> 1010 us (1.091)
  waiting for transfers between devices: 249 us -> 370 us
  blocking collectives: 155 us -> 114 us
    reduce_scatter x1, waiting for transfers between devices: 8.77 us -> 89.3 us  [body(): lax.psum_scatter(grad_zx_w, 'dp', scatter_dimension=0, tiled=True)]
    psum x1 -> x0, blocking collectives: 40.8 us -> none  [body(): grad_bc_in = lax.psum(grad_bc_part, 'tensor').astype(jnp.bfloat16)]
    reduce_scatter x1, waiting for transfers between devices: 0.01 us -> 40.1 us  [body(): lax.psum_scatter(grad_out_w, 'dp', scatter_dimension=0, tiled=True)]
    unnamed x119 -> x113, local copies, waits for them, and re-layouts: 28.6 us -> 24.6 us
  transfers between devices with their start and end apart: 10 -> 11, of which waited for: 6 -> 7; matrix products, arithmetic and copies ran while one was open for 53% -> 25% of each run, Pallas kernels for 0% -> 0%
where the time goes in v1:
time: 1010 us
  waiting for transfers between devices  370 us (37%)
  matrix products  237 us (23%)
  other arithmetic  148 us (15%)
  local copies, waits for them, and re-layouts  119 us (12%)
  blocking collectives  114 us (11%)
  between operations  14.8 us (1%)
    reduce_scatter x1, waiting for transfers between devices, body(): lax.psum_scatter(grad_zx_w, 'dp', scatter_dimension=0, tiled=True)  89.3 us
    dot_general x24, matrix products, step_block(): jnp.einsum('ijh,jhp->ihp', weights, x_block, precision=FULL_PRECISION)  78.3 us
    reduce_scatter x1, waiting for transfers between devices, body(): lax.psum_scatter(from_zx + lax.dot_general(grad_dt_low, dt_full, CONTRACT...  71.4 us
    reduce_scatter x1, waiting for transfers between devices, body(): lax.psum_scatter(grad_bc_w, 'dp', scatter_dimension=0, tiled=True)  67.3 us
    reduce_scatter x1, waiting for transfers between devices, body(): lax.psum_scatter(grad_dt_w, 'dp', scatter_dimension=0, tiled=True)  54.1 us
    psum x1, blocking collectives, body(): lax.psum((grad_norm_gain, widen(grad_x_taps, chan_start, total_channels),...  41.2 us
    reduce_scatter x1, waiting for transfers between devices, body(): lax.psum_scatter(grad_out_w, 'dp', scatter_dimension=0, tiled=True)  40.1 us
    another operation x73, other arithmetic  39.1 us
  transfers between devices with their start and end apart: 11, of which 7 were waited for; matrix products, arithmetic and copies ran while one was open for 25% of the time, Pallas kernels for 0%

profile of v1, /device:TPU:0, one launch (start us, length us, event | category | flops | bytes accessed | tf_op | source)
XLA Modules:
  0.0 1005.0 jit_solution(12777710000781962726)
XLA Ops:
  16.2 27.9 %all_gather.25 = bf16[1024,8]{0,1:T(8,128)(2,1)S(1)} all-gather(bf16[128,8]{0,1:T(8,128)(2,1)S(1)} %copy-done.46), channel_id=1, replica_groups=mesh['dp'=8,'tensor'=4] {'dp'}, dimensions={0}, use_global_device_ids=true | all-gather | bytes 18432 | tf_op jit(solution)/shard_map/all_gather | solution.py:123
  44.2 32.4 %all_gather.27 = bf16[1024,256]{1,0:T(8,128)(2,1)S(1)} all-gather(bf16[128,256]{1,0:T(8,128)(2,1)S(1)} %copy-done.17), channel_id=1, replica_groups=mesh['dp'=8,'tensor'=4] {'dp'}, dimensions={0}, use_global_device_ids=true | all-gather | bytes 589824 | tf_op jit(solution)/shard_map/all_gather | solution.py:122
  77.6 3.8 fusion.161
  86.3 15.2 %all-gather.10.cloned.1.call-done = bf16[1024,2,512]{2,0,1:T(8,128)(2,1)} async-done(((bf16[128,2,512]{2,0,1:T(8,128)(2,1)}), bf16[1024,2,512]{2,0,1:T(8,128)(2,1)}) %all-gather.10.cloned.1.call-update) | async-done | bytes 2097168 | tf_op jit(solution)/shard_map/all_gather | solution.py:121
  101.5 7.1 fusion.109
  111.8 4.7 fusion.123
  116.5 7.1 reshape.373
  123.6 6.8 copy.89
  130.4 4.0 compare_select_fusion.2
  136.9 87.5 %while.43 = (s32[]{:T(128)}, f32[8,64,128]{2,1,0:T(8,128)S(1)}, f32[8,256,8,64]{1,3,2,0:T(8,128)}, f32[8,8,64,128]{3,2,1,0:T(8,128)}, f32[8,256,8]{1,2,0:T(8,128...) while((s32[]{:T(128)}, f32[8,64,128]{2,1,0:T(8,128)S(1)}, ...), condition=%wide.region_4.5_spmd.clone.clone, body=%wide.region_1.4_spmd.clone.clone.sunk | while | flops 909711360 | bytes 5641051 | solution.py:56
  139.5 3.6 fusion.270
  150.5 3.6 fusion.270
  161.4 3.6 fusion.270
  172.3 3.6 fusion.270
  183.2 3.6 fusion.270
  194.2 3.6 fusion.270
  205.1 3.6 fusion.270
  216.0 3.6 fusion.270
  224.4 6.9 copy.101
  231.3 7.5 reshape.370
  238.8 7.4 multiply_reduce_fusion.8
  246.2 5.7 psum.77
  252.1 7.4 fusion.96
  259.5 6.7 psum.78
  266.2 11.4 %multiply_reduce_fusion.3 = (f32[512]{0:T(512)}, f32[2048,512]{1,0:T(8,128)}, bf16[2048,1,512]{2,0,1:T(8,128)(2,1)}) fusion(f32[2048,512]{1,0:T(8,128)} %get-tuple-element.766, f32[2048,2,512]{2,0,1:T(8,128)} %copy-done.1, f32[2048]{0:T(1024)S(1)} %broadcast_multiply_fusion.8, f32[2048,512]{1,0:T(8,128)} %get-tuple-element.762, ...), kind=kLoop, calls=%fused_computation.161 | loop fusion | flops 30408192 | bytes 25196544 | tf_op jit(solution)/shard_map/transpose(jvp())/reduce_sum | solution.py:83
  277.7 7.0 reshape.371
  284.7 6.8 copy.94
  296.8 198.2 %while.42 = (s32[]{:T(128)}, f32[8]{0:T(128)}, f32[8,64,128]{2,1,0:T(8,128)S(1)}, f32[8,256,8,64]{1,3,2,0:T(8,128)}, f32[8,256,8]{1,2,0:T(8,128)}, /*index=5*/f3...) while((s32[]{:T(128)}, f32[8]{0:T(128)}, ...), condition=%wide.region_24.25_spmd.clone, body=%wide.region_10.0_spmd.clone.sunk | while | flops 2126610432 | bytes 15952340 | solution.py:56
  495.0 6.2 multiply_reduce_fusion.12
  503.9 7.3 fusion.130
  511.3 7.2 copy.104
  518.4 7.5 reshape.372
  526.0 11.5 %multiply_reduce_fusion.6 = (f32[512]{0:T(512)S(1)}, f32[512]{0:T(512)S(1)}, f32[512]{0:T(512)S(1)}, f32[512]{0:T(512)S(1)}, f32[512]{0:T(512)S(1)}, /*index=5*/f32[2048,512]{1,0:T(8,128)S(1)}) fusion(f32[2048,512]{1,0:T(8,128)} %copy-done, f32[2048,2,512]{2,0,1:T(8,128)} %copy-done.1, f32[2048,512]{1,0:T(8,128)} %get-tuple-element.766, ...), kind=kLoop, calls=%fused_computation.164 | loop fusion | flops 20968960 | bytes 25178112 | tf_op jit(solution)/shard_map/transpose(jvp())/reduce_sum | solution.py:19
  537.5 5.8 broadcast_multiply_fusion
  543.3 7.1 fusion.127
  550.5 8.3 fusion.107
  562.7 6.8 bitcast_add_fusion
  570.7 7.8 fusion.148
  582.2 4.4 reduce_sum.410
  586.7 5.0 fusion.162
  593.1 40.1 %reduce-scatter.17.cloned.1.call-done = f32[128,512]{0,1:T(8,128)} async-done(((f32[1024,512]{0,1:T(8,128)}), f32[128,512]{0,1:T(8,128)}) %reduce-scatter.17.cloned.1.call-update) | async-done | bytes 262160 | tf_op jit(solution)/shard_map/reduce_scatter | solution.py:226
  634.9 89.3 %reduce-scatter.11.cloned.1.call-done = f32[128,2,512]{2,0,1:T(8,128)} async-done(((f32[1024,2,512]{2,0,1:T(8,128)}), f32[128,2,512]{2,0,1:T(8,128)}) %reduce-scatter.11.cloned.1.call-update) | async-done | bytes 524304 | tf_op jit(solution)/shard_map/reduce_scatter | solution.py:223
  726.5 71.4 %reduce-scatter.9.cloned.1.call-done = f32[512,1024]{1,0:T(8,128)} async-done(((f32[2048,1024]{1,0:T(8,128)}), f32[512,1024]{1,0:T(8,128)}) %reduce-scatter.9.cloned.1.call-update) | async-done | bytes 2097168 | tf_op jit(solution)/shard_map/reduce_scatter | solution.py:209
  800.6 41.2 %all-reduce.19 = (f32[1024]{0:T(1024)}, f32[4,2048]{1,0:T(4,128)}, f32[2048]{0:T(1024)}, f32[4,256]{1,0:T(4,128)}, f32[256]{0:T(256)}, /*index=5*/f32[32]{0:T(128)}, f32[32]{0:T(128)}, f32[32]{0:T(128)}, f32[2048]{0:T(1024)}) all-reduce(f32[1024]{0:T(1024)S(1)} %get-tuple-element.689, ...), channel_id=1, replica_groups=mesh['dp'=8,'tensor'=4] {'dp','tensor'}, use_global_device_ids=true, to_apply=%region_29.30 | all-reduce | flops 14688 | bytes 117504 | tf_op jit(solution)/shard_map/psum | solution.py:228
  841.8 30.9 %reduce-scatter.7.cloned.1.call-done = f32[512,1024]{1,0:T(8,128)} async-done(((f32[2048,1024]{1,0:T(8,128)}), f32[512,1024]{1,0:T(8,128)}) %reduce-scatter.7.cloned.1.call-update) | async-done | bytes 2097168 | tf_op jit(solution)/shard_map/reduce_scatter | solution.py:159
  872.7 4.3 fusion.122
  876.9 54.1 %reduce-scatter.15.cloned.1.call-done = f32[128,8]{0,1:T(8,128)} async-done(((f32[1024,8]{0,1:T(8,128)}), f32[128,8]{0,1:T(8,128)}) %reduce-scatter.15.cloned.1.call-update) | async-done | bytes 4112 | tf_op jit(solution)/shard_map/reduce_scatter | solution.py:225
  931.0 67.3 %reduce-scatter.13.cloned.1.call-done = f32[128,256]{1,0:T(8,128)} async-done(((f32[1024,256]{1,0:T(8,128)}), f32[128,256]{1,0:T(8,128)}) %reduce-scatter.13.cloned.1.call-update) | async-done | bytes 131088 | tf_op jit(solution)/shard_map/reduce_scatter | solution.py:224
  (596 shorter events, 300.8 us)
Async XLA Ops:
  7.2 6.4 copy-start.49
  7.2 7.1 copy-start.52
  7.2 7.2 copy-start.53
  7.2 8.9 copy-start.45
  7.2 8.9 copy-start.46
  7.2 36.9 %copy-start.17 = (bf16[128,256]{1,0:T(8,128)(2,1)S(1)}, bf16[128,256]{1,0:T(8,128)(2,1)}, u32[]{:S(2)}) copy-start(bf16[128,256]{1,0:T(8,128)(2,1)} %param.23) | copy-start | bytes 196612
  7.3 70.3 %all-gather.8.cloned.1.call-start = ((), (), s32[]{:S(2)}) async-start(), calls=%async_computation.6 | async-start | bytes 5242880 | tf_op jit(solution)/shard_map/all_gather | solution.py:128
  8.9 7.3 copy-start.33
  8.9 7.3 copy-start.21
  11.4 90.1 %all-gather.10.cloned.1.call-start = ((), (), s32[]{:S(2)}) async-start(), calls=%async_computation.7 | async-start | bytes 2359296 | tf_op jit(solution)/shard_map/all_gather | solution.py:121
  12.2 239.8 %all-gather.12.cloned.1.call-start = ((), (), s32[]{:S(2)}) async-start(), calls=%async_computation.8 | async-start | bytes 1179648 | tf_op jit(solution)/shard_map/all_gather | solution.py:124
  13.0 239.1 %all-gather.14.cloned.1.call-start = ((), (), s32[]{:S(2)}) async-start(), calls=%async_computation.15 | async-start | bytes 5242880 | tf_op jit(solution)/shard_map/all_gather | solution.py:167
  13.6 568.6 %all-gather.16.cloned.1.call-start = ((), (), s32[]{:S(2)}) async-start(), calls=%async_computation.16 | async-start | bytes 10485760 | tf_op jit(solution)/shard_map/all_gather | solution.py:195
  15.2 251.0 %copy-start.23 = (f32[512]{0:T(512)}, f32[512]{0:T(512)S(1)}, u32[]{:S(2)}) copy-start(f32[512]{0:T(512)S(1)} %dynamic_slice.100) | copy-start | bytes 6148
  16.1 250.1 %copy-start.19 = (f32[512]{0:T(512)}, f32[512]{0:T(512)S(1)}, u32[]{:S(2)}) copy-start(f32[512]{0:T(512)S(1)} %mul.863) | copy-start | bytes 6148
  16.2 65.2 %copy-start.36 = (f32[1,256]{1,0:T(1,128)}, f32[1,256]{1,0:T(1,128)S(1)}, u32[]{:S(2)}) copy-start(f32[1,256]{1,0:T(1,128)S(1)} %get-tuple-element.793) | copy-start | bytes 3076
  16.2 65.2 %copy-start.38 = (f32[1,256]{1,0:T(1,128)}, f32[1,256]{1,0:T(1,128)S(1)}, u32[]{:S(2)}) copy-start(f32[1,256]{1,0:T(1,128)S(1)} %get-tuple-element.794) | copy-start | bytes 3076
  16.2 65.2 %copy-start.40 = (f32[1,256]{1,0:T(1,128)}, f32[1,256]{1,0:T(1,128)S(1)}, u32[]{:S(2)}) copy-start(f32[1,256]{1,0:T(1,128)S(1)} %get-tuple-element.795) | copy-start | bytes 3076
  16.2 65.2 %copy-start.42 = (f32[1,256]{1,0:T(1,128)}, f32[1,256]{1,0:T(1,128)S(1)}, u32[]{:S(2)}) copy-start(f32[1,256]{1,0:T(1,128)S(1)} %get-tuple-element.796) | copy-start | bytes 3076
  44.1 86.3 %copy-start.15 = (bf16[1024,8]{0,1:T(8,128)(2,1)}, bf16[1024,8]{0,1:T(8,128)(2,1)S(1)}, u32[]{:S(2)}) copy-start(bf16[1024,8]{0,1:T(8,128)(2,1)S(1)} %all_gather.25) | copy-start | bytes 49156
  44.1 37.3 %copy-start.48 = (f32[256]{0:T(256)S(1)}, f32[256]{0:T(256)}, u32[]{:S(2)}) copy-start(f32[256]{0:T(256)} %param.29) | copy-start | bytes 3076
  77.5 34.3 %copy-start.25 = (f32[1,512]{1,0:T(1,128)}, f32[1,512]{1,0:T(1,128)S(1)}, u32[]{:S(2)}) copy-start(f32[1,512]{1,0:T(1,128)S(1)} %get-tuple-element.787) | copy-start | bytes 6148
  77.5 34.3 %copy-start.27 = (f32[1,512]{1,0:T(1,128)}, f32[1,512]{1,0:T(1,128)S(1)}, u32[]{:S(2)}) copy-start(f32[1,512]{1,0:T(1,128)S(1)} %get-tuple-element.788) | copy-start | bytes 6148
  77.6 34.2 %copy-start.29 = (f32[1,512]{1,0:T(1,128)}, f32[1,512]{1,0:T(1,128)S(1)}, u32[]{:S(2)}) copy-start(f32[1,512]{1,0:T(1,128)S(1)} %get-tuple-element.789) | copy-start | bytes 6148
  77.6 34.2 %copy-start.31 = (f32[1,512]{1,0:T(1,128)}, f32[1,512]{1,0:T(1,128)S(1)}, u32[]{:S(2)}) copy-start(f32[1,512]{1,0:T(1,128)S(1)} %get-tuple-element.790) | copy-start | bytes 6148
  252.0 14.2 %copy-start.13 = (f32[2048]{0:T(1024)}, f32[2048]{0:T(1024)S(1)}, u32[]{:S(2)}) copy-start(f32[2048]{0:T(1024)S(1)} %get-tuple-element.792) | copy-start | bytes 24580
  495.0 6.3 copy-start.37
  495.0 6.3 copy-start.39
  495.0 6.3 copy-start.41
  495.0 6.3 copy-start.43
  503.9 129.3 %reduce-scatter.17.cloned.1.call-start = ((), (), s32[]{:S(2)}) async-start(), calls=%async_computation.14 | async-start | bytes 2359296 | tf_op jit(solution)/shard_map/reduce_scatter | solution.py:226
  511.2 213.0 %reduce-scatter.11.cloned.1.call-start = ((), (), s32[]{:S(2)}) async-start(), calls=%async_computation.11 | async-start | bytes 4718592 | tf_op jit(solution)/shard_map/reduce_scatter | solution.py:223
  518.4 7.5 copy-start.20
  525.9 11.5 %copy-start.26 = (f32[1,512]{1,0:T(1,128)S(1)}, f32[1,512]{1,0:T(1,128)}, u32[]{:S(2)}) copy-start(f32[1,512]{1,0:T(1,128)} %copy-done.25) | copy-start | bytes 6148
  525.9 11.5 %copy-start.28 = (f32[1,512]{1,0:T(1,128)S(1)}, f32[1,512]{1,0:T(1,128)}, u32[]{:S(2)}) copy-start(f32[1,512]{1,0:T(1,128)} %copy-done.27) | copy-start | bytes 6148
  525.9 11.5 %copy-start.30 = (f32[1,512]{1,0:T(1,128)S(1)}, f32[1,512]{1,0:T(1,128)}, u32[]{:S(2)}) copy-start(f32[1,512]{1,0:T(1,128)} %copy-done.29) | copy-start | bytes 6148
  525.9 11.5 %copy-start.32 = (f32[1,512]{1,0:T(1,128)S(1)}, f32[1,512]{1,0:T(1,128)}, u32[]{:S(2)}) copy-start(f32[1,512]{1,0:T(1,128)} %copy-done.31) | copy-start | bytes 6148
  543.3 7.2 copy-start.2
  558.8 239.1 %reduce-scatter.9.cloned.1.call-start = ((), (), s32[]{:S(2)}) async-start(), calls=%async_computation.10 | async-start | bytes 10485760 | tf_op jit(solution)/shard_map/reduce_scatter | solution.py:209
  569.5 303.1 %reduce-scatter.7.cloned.1.call-start = ((), (), s32[]{:S(2)}) async-start(), calls=%async_computation.9 | async-start | bytes 10485760 | tf_op jit(solution)/shard_map/reduce_scatter | solution.py:159
  578.6 352.4 %reduce-scatter.15.cloned.1.call-start = ((), (), s32[]{:S(2)}) async-start(), calls=%async_computation.13 | async-start | bytes 36864 | tf_op jit(solution)/shard_map/reduce_scatter | solution.py:225
  582.1 416.2 %reduce-scatter.13.cloned.1.call-start = ((), (), s32[]{:S(2)}) async-start(), calls=%async_computation.12 | async-start | bytes 1179648 | tf_op jit(solution)/shard_map/reduce_scatter | solution.py:224
  586.6 6.3 copy-start.35
  586.6 6.3 copy-start.50
  586.6 211.3 %copy-start.3 = (bf16[1,512,1024]{2,1,0:T(8,128)(2,1)S(1)}, bf16[1,512,1024]{2,1,0:T(8,128)(2,1)}, u32[]{:S(2)}) copy-start(bf16[1,512,1024]{2,1,0:T(8,128)(2,1)} %param.19) | copy-start | bytes 3145732
  586.6 211.3 %copy-start.18 = (f32[1024]{0:T(1024)S(1)}, f32[1024]{0:T(1024)}, u32[]{:S(2)}) copy-start(f32[1024]{0:T(1024)} %param.21) | copy-start | bytes 12292
  586.7 211.3 %copy-start.22 = (f32[512]{0:T(512)S(1)}, f32[512]{0:T(512)}, u32[]{:S(2)}) copy-start(f32[512]{0:T(512)} %copy-done.21) | copy-start | bytes 6148
  591.6 250.2 %copy-start.34 = (f32[512]{0:T(512)S(1)}, f32[512]{0:T(512)}, u32[]{:S(2)}) copy-start(f32[512]{0:T(512)} %copy-done.33) | copy-start | bytes 6148
  (17 other events, 50.9 us)
Sparse Core Ops, SparseCore 0:
  11.6 37.1 all-gather.7
  51.5 49.9 all-gather.9
  103.6 38.7 all-gather.11
  143.9 33.0 all-gather.13
  504.0 56.4 all-gather.15
  563.8 69.2 reduce-scatter.16
  636.7 87.4 reduce-scatter.10
  726.8 71.0 reduce-scatter.8
  800.5 72.1 reduce-scatter.6
  876.2 54.7 reduce-scatter.14
  935.0 63.2 reduce-scatter.12
